TPU v7x, 32 devices: a whole 2x2x4 slice. The times are simulated.
32 devices in a mesh: grp: 2 (over core), tile: 16 (over z, y, x).
Axes of the slice: x: 2, y: 2, z: 4, core: 2. Of those that a mesh axis runs over, the one named last changes fastest.
Arguments:
- attn_input: bfloat16 [2048, 4096], P(('grp', 'tile')), may hold values from -9 to 9
- mlp_input: bfloat16 [2048, 4096], P(('grp', 'tile')), may hold values from -9 to 9
Outputs:
- hess_attn: float32 [16, 1024, 1024], P('tile', 'grp')
- hess_mlp: float32 [16, 1024, 1024], P('tile', 'grp')
All inputs are finite; a program needn't handle non-finite values.
Results may differ from a plain program's by a relative error of at most 0.0003.
Values may be sent and summed in bfloat16 or wider, within the bound.
A program may use at most 192 MiB of HBM per device.

v0:
```python
import jax
import jax.numpy as jnp
from jax import lax
from jax.sharding import PartitionSpec as P

ROWB = 4
TOKB = 32


def tile_first(inputs, tile_count):
    tok_rows, feat_width = inputs.shape
    col_blocks = tile_count // ROWB
    row_width = feat_width // ROWB
    col_width = feat_width // col_blocks

    def accumulate(turn_idx, partial_value):
        tok_block = lax.dynamic_slice_in_dim(inputs, turn_idx * TOKB, TOKB, 0)
        row_parts = tok_block.reshape(TOKB, ROWB, row_width).transpose(1, 0, 2)
        row_send = jnp.repeat(row_parts, col_blocks, axis=0)
        col_parts = tok_block.reshape(TOKB, col_blocks, col_width).transpose(1, 0, 2)
        col_send = jnp.tile(col_parts, (ROWB, 1, 1))
        rows_in, cols_in = (
            lax.all_to_all(row_send, "tile", split_axis=0, concat_axis=0, tiled=True),
            lax.all_to_all(col_send, "tile", split_axis=0, concat_axis=0, tiled=True),
        )
        rows_flat = rows_in.reshape(tile_count * TOKB, row_width)
        cols_flat = cols_in.reshape(tile_count * TOKB, col_width)
        return partial_value + lax.dot_general(
            rows_flat, cols_flat, (((0,), (0,)), ((), ())), preferred_element_type=jnp.float32
        )

    partial_value = lax.fori_loop(
        0, tok_rows // TOKB, accumulate, jnp.zeros((row_width, col_width), jnp.float32)
    )
    shares = lax.psum_scatter(partial_value, "grp", scatter_dimension=0, tiled=True)
    return shares[None]


def hessian_share(inputs):
    tile_count = lax.axis_size("tile")
    group_count = lax.axis_size("grp")
    norm_factor = 2.0 / (inputs.shape[0] * tile_count * group_count)
    shares = tile_first(inputs, tile_count)
    return shares * norm_factor


def body(attn_input, mlp_input):
    return (hessian_share(attn_input), hessian_share(mlp_input))


def solution(mesh):
    in_specs = (P(("grp", "tile"), None), P(("grp", "tile"), None))
    out_specs = (P("tile", "grp", None), P("tile", "grp", None))
    return jax.shard_map(body, mesh=mesh, in_specs=in_specs, out_specs=out_specs, check_vma=False)
```

profile of v0, /device:TPU:0, one launch (start us, length us, event | category | flops | bytes accessed | tf_op | source)
XLA Modules:
  0.0 291.0 jit_solution(9503920627443665375)
XLA Ops:
  7.2 133.3 %while.29 = (s32[]{:T(128)}, f32[1024,1024]{1,0:T(8,128)}, bf16[64,4096]{1,0:T(8,128)(2,1)}, s32[]{:T(128)}, s32[]{:T(128)}, /*index=5*/s32[]{:T(128)}, s32[]{:T(128)}) while((s32[]{:T(128)}, f32[1024,1024]{1,0:T(8,128)}, bf16[64,4096]{1,0:T(8,128)(2,1)}, s32[]{:T(128)}, s32[]{:T(128)}, /*index=5*/s32[]{:T(128)}, s32[]{:T(128)}) %tuple.66), condition=%wide.region_4.0_spmd.clone, body=%wide.region_3.0_spmd.clone.sunk | while | flops 1075838976 | bytes 19923112 | solution.py:32
  8.6 34.5 %all_to_all.45 = bf16[16,32,1024]{2,1,0:T(8,128)(2,1)S(1)} all-to-all(bf16[16,32,1024]{2,1,0:T(8,128)(2,1)S(1)} %bitcast.42), channel_id=1, replica_groups=mesh['grp'=2,'tile'=16] {'tile'}, dimensions={0} | all-to-all | bytes 2097152 | tf_op jit(solution)/shard_map/while/body/eval_jaxpr/all_to_all | solution.py:24
  43.1 1.1 broadcast_in_dim.21
  44.2 3.9 %all-to-all-start.2 = ((bf16[16,32,1024]{2,1,0:T(8,128)(2,1)}), bf16[16,32,1024]{2,1,0:T(8,128)(2,1)S(1)}, u32[]{:S(2)}, u32[]{:S(2)}) async-start(bf16[16,32,1024]{2,1,0:T(8,128)(2,1)} %bitcast.40), calls=%async_computation.2 | async-start | bytes 2097152 | tf_op jit(solution)/shard_map/while/body/eval_jaxpr/all_to_all | solution.py:23
  48.1 23.7 %all-to-all-done.2 = bf16[16,32,1024]{2,1,0:T(8,128)(2,1)S(1)} async-done(((bf16[16,32,1024]{2,1,0:T(8,128)(2,1)}), bf16[16,32,1024]{2,1,0:T(8,128)(2,1)S(1)}, u32[]{:S(2)}, u32[]{:S(2)}) %all-to-all-start.2) | async-done | bytes 1048608 | tf_op jit(solution)/shard_map/while/body/eval_jaxpr/all_to_all | solution.py:23
  71.8 3.3 %bitcast_add_fusion.5 = f32[1024,1024]{1,0:T(8,128)} fusion(f32[1024,1024]{1,0:T(8,128)} %get-tuple-element.235, bf16[16,32,1024]{2,1,0:T(8,128)(2,1)S(1)} %all-to-all-done.2, bf16[16,32,1024]{2,1,0:T(8,128)(2,1)S(1)} %all_to_all.45, pred[]{:T(512)S(6)} %compare.7), kind=kOutput, calls=%fused_computation.2.clone.1 | convolution fusion | flops 1075838976 | bytes 10485761 | tf_op jit(solution)/shard_map/while/body/eval_jaxpr/dot_general | solution.py:28
  76.5 30.7 %all_to_all.45 = bf16[16,32,1024]{2,1,0:T(8,128)(2,1)S(1)} all-to-all(bf16[16,32,1024]{2,1,0:T(8,128)(2,1)S(1)} %bitcast.42), channel_id=1, replica_groups=mesh['grp'=2,'tile'=16] {'tile'}, dimensions={0} | all-to-all | bytes 2097152 | tf_op jit(solution)/shard_map/while/body/eval_jaxpr/all_to_all | solution.py:24
  107.1 1.1 broadcast_in_dim.21
  108.2 3.9 %all-to-all-start.2 = ((bf16[16,32,1024]{2,1,0:T(8,128)(2,1)}), bf16[16,32,1024]{2,1,0:T(8,128)(2,1)S(1)}, u32[]{:S(2)}, u32[]{:S(2)}) async-start(bf16[16,32,1024]{2,1,0:T(8,128)(2,1)} %bitcast.40), calls=%async_computation.2 | async-start | bytes 2097152 | tf_op jit(solution)/shard_map/while/body/eval_jaxpr/all_to_all | solution.py:23
  112.1 23.0 %all-to-all-done.2 = bf16[16,32,1024]{2,1,0:T(8,128)(2,1)S(1)} async-done(((bf16[16,32,1024]{2,1,0:T(8,128)(2,1)}), bf16[16,32,1024]{2,1,0:T(8,128)(2,1)S(1)}, u32[]{:S(2)}, u32[]{:S(2)}) %all-to-all-start.2) | async-done | bytes 1048608 | tf_op jit(solution)/shard_map/while/body/eval_jaxpr/all_to_all | solution.py:23
  135.1 5.5 %bitcast_add_fusion.5 = f32[1024,1024]{1,0:T(8,128)} fusion(f32[1024,1024]{1,0:T(8,128)} %get-tuple-element.235, bf16[16,32,1024]{2,1,0:T(8,128)(2,1)S(1)} %all-to-all-done.2, bf16[16,32,1024]{2,1,0:T(8,128)(2,1)S(1)} %all_to_all.45, pred[]{:T(512)S(6)} %compare.7), kind=kOutput, calls=%fused_computation.2.clone.1 | convolution fusion | flops 1075838976 | bytes 10485761 | tf_op jit(solution)/shard_map/while/body/eval_jaxpr/dot_general | solution.py:28
  141.6 126.8 %while.28 = (s32[]{:T(128)}, f32[1024,1024]{1,0:T(8,128)}, bf16[64,4096]{1,0:T(8,128)(2,1)S(1)}, s32[]{:T(128)}, s32[]{:T(128)}, /*index=5*/s32[]{:T(128)}, s32[]{:T(128)}) while((s32[]{:T(128)}, f32[1024,1024]{1,0:T(8,128)}, bf16[64,4096]{1,0:T(8,128)(2,1)S(1)}, s32[]{:T(128)}, s32[]{:T(128)}, /*index=5*/s32[]{:T(128)}, ...), condition=%wide.region_1.0_spmd.clone, body=%wide.region_0.0_spmd.clone.sunk | while | flops 1075838976 | bytes 19923112 | solution.py:32
  142.0 30.7 %all_to_all.44 = bf16[16,32,1024]{2,1,0:T(8,128)(2,1)S(1)} all-to-all(bf16[16,32,1024]{2,1,0:T(8,128)(2,1)S(1)} %bitcast.43), channel_id=1, replica_groups=mesh['grp'=2,'tile'=16] {'tile'}, dimensions={0} | all-to-all | bytes 2097152 | tf_op jit(solution)/shard_map/while/body/eval_jaxpr/all_to_all | solution.py:24
  172.8 1.1 broadcast_in_dim.20
  173.9 3.9 %all-to-all-start = ((bf16[16,32,1024]{2,1,0:T(8,128)(2,1)}), bf16[16,32,1024]{2,1,0:T(8,128)(2,1)S(1)}, u32[]{:S(2)}, u32[]{:S(2)}) async-start(bf16[16,32,1024]{2,1,0:T(8,128)(2,1)} %bitcast.34), calls=%async_computation | async-start | bytes 2097152 | tf_op jit(solution)/shard_map/while/body/eval_jaxpr/all_to_all | solution.py:23
  177.8 22.9 %all-to-all-done = bf16[16,32,1024]{2,1,0:T(8,128)(2,1)S(1)} async-done(((bf16[16,32,1024]{2,1,0:T(8,128)(2,1)}), bf16[16,32,1024]{2,1,0:T(8,128)(2,1)S(1)}, u32[]{:S(2)}, u32[]{:S(2)}) %all-to-all-start) | async-done | bytes 1048608 | tf_op jit(solution)/shard_map/while/body/eval_jaxpr/all_to_all | solution.py:23
  200.7 3.2 %bitcast_add_fusion.4 = f32[1024,1024]{1,0:T(8,128)} fusion(f32[1024,1024]{1,0:T(8,128)} %get-tuple-element.214, bf16[16,32,1024]{2,1,0:T(8,128)(2,1)S(1)} %all-to-all-done, bf16[16,32,1024]{2,1,0:T(8,128)(2,1)S(1)} %all_to_all.44, pred[]{:T(512)S(6)} %compare.6), kind=kOutput, calls=%fused_computation.clone.1 | convolution fusion | flops 1075838976 | bytes 10485761 | tf_op jit(solution)/shard_map/while/body/eval_jaxpr/dot_general | solution.py:28
  204.3 30.7 %all_to_all.44 = bf16[16,32,1024]{2,1,0:T(8,128)(2,1)S(1)} all-to-all(bf16[16,32,1024]{2,1,0:T(8,128)(2,1)S(1)} %bitcast.43), channel_id=1, replica_groups=mesh['grp'=2,'tile'=16] {'tile'}, dimensions={0} | all-to-all | bytes 2097152 | tf_op jit(solution)/shard_map/while/body/eval_jaxpr/all_to_all | solution.py:24
  236.1 3.9 %all-to-all-start = ((bf16[16,32,1024]{2,1,0:T(8,128)(2,1)}), bf16[16,32,1024]{2,1,0:T(8,128)(2,1)S(1)}, u32[]{:S(2)}, u32[]{:S(2)}) async-start(bf16[16,32,1024]{2,1,0:T(8,128)(2,1)} %bitcast.34), calls=%async_computation | async-start | bytes 2097152 | tf_op jit(solution)/shard_map/while/body/eval_jaxpr/all_to_all | solution.py:23
  240.0 22.9 %all-to-all-done = bf16[16,32,1024]{2,1,0:T(8,128)(2,1)S(1)} async-done(((bf16[16,32,1024]{2,1,0:T(8,128)(2,1)}), bf16[16,32,1024]{2,1,0:T(8,128)(2,1)S(1)}, u32[]{:S(2)}, u32[]{:S(2)}) %all-to-all-start) | async-done | bytes 1048608 | tf_op jit(solution)/shard_map/while/body/eval_jaxpr/all_to_all | solution.py:23
  262.9 5.4 %bitcast_add_fusion.4 = f32[1024,1024]{1,0:T(8,128)} fusion(f32[1024,1024]{1,0:T(8,128)} %get-tuple-element.214, bf16[16,32,1024]{2,1,0:T(8,128)(2,1)S(1)} %all-to-all-done, bf16[16,32,1024]{2,1,0:T(8,128)(2,1)S(1)} %all_to_all.44, pred[]{:T(512)S(6)} %compare.6), kind=kOutput, calls=%fused_computation.clone.1 | convolution fusion | flops 1075838976 | bytes 10485761 | tf_op jit(solution)/shard_map/while/body/eval_jaxpr/dot_general | solution.py:28
  268.4 3.2 %multiply_bitcast_fusion = f32[1,512,1024]{2,1,0:T(8,128)} fusion(f32[512,1024]{1,0:T(8,128)} %reduce-scatter.5.cloned.1.call-done), kind=kLoop, calls=%fused_computation.4 | loop fusion | flops 524288 | bytes 4194304 | tf_op jit(solution)/shard_map/mul | solution.py:44
  271.6 9.3 %reduce-scatter.3.cloned.1.call-done = f32[512,1024]{1,0:T(8,128)} async-done(((f32[1024,1024]{1,0:T(8,128)}), f32[512,1024]{1,0:T(8,128)}) %reduce-scatter.3.cloned.1.call-update) | async-done | bytes 2097168 | tf_op jit(solution)/shard_map/reduce_scatter | solution.py:35
  281.0 3.2 %multiply_bitcast_fusion.1 = f32[1,512,1024]{2,1,0:T(8,128)} fusion(f32[512,1024]{1,0:T(8,128)} %reduce-scatter.3.cloned.1.call-done), kind=kLoop, calls=%fused_computation.5 | loop fusion | flops 524288 | bytes 4194304 | tf_op jit(solution)/shard_map/mul | solution.py:44
  (26 shorter events, 5.7 us)
Async XLA Ops:
  7.2 261.3 %reduce-scatter.5.cloned.1.call-start = ((), (), s32[]{:S(2)}) async-start(), calls=%async_computation.7 | async-start | bytes 6291456 | tf_op jit(solution)/shard_map/reduce_scatter | solution.py:35
  44.2 27.6 %all-to-all-start.2 = ((bf16[16,32,1024]{2,1,0:T(8,128)(2,1)}), bf16[16,32,1024]{2,1,0:T(8,128)(2,1)S(1)}, u32[]{:S(2)}, u32[]{:S(2)}) async-start(bf16[16,32,1024]{2,1,0:T(8,128)(2,1)} %bitcast.40), calls=%async_computation.2 | async-start | bytes 2097152 | tf_op jit(solution)/shard_map/while/body/eval_jaxpr/all_to_all | solution.py:23
  108.2 26.9 %all-to-all-start.2 = ((bf16[16,32,1024]{2,1,0:T(8,128)(2,1)}), bf16[16,32,1024]{2,1,0:T(8,128)(2,1)S(1)}, u32[]{:S(2)}, u32[]{:S(2)}) async-start(bf16[16,32,1024]{2,1,0:T(8,128)(2,1)} %bitcast.40), calls=%async_computation.2 | async-start | bytes 2097152 | tf_op jit(solution)/shard_map/while/body/eval_jaxpr/all_to_all | solution.py:23
  140.6 1.0 copy-start
  140.6 140.4 %reduce-scatter.3.cloned.1.call-start = ((), (), s32[]{:S(2)}) async-start(), calls=%async_computation.6 | async-start | bytes 6291456 | tf_op jit(solution)/shard_map/reduce_scatter | solution.py:35
  173.9 26.8 %all-to-all-start = ((bf16[16,32,1024]{2,1,0:T(8,128)(2,1)}), bf16[16,32,1024]{2,1,0:T(8,128)(2,1)S(1)}, u32[]{:S(2)}, u32[]{:S(2)}) async-start(bf16[16,32,1024]{2,1,0:T(8,128)(2,1)} %bitcast.34), calls=%async_computation | async-start | bytes 2097152 | tf_op jit(solution)/shard_map/while/body/eval_jaxpr/all_to_all | solution.py:23
  236.1 26.8 %all-to-all-start = ((bf16[16,32,1024]{2,1,0:T(8,128)(2,1)}), bf16[16,32,1024]{2,1,0:T(8,128)(2,1)S(1)}, u32[]{:S(2)}, u32[]{:S(2)}) async-start(bf16[16,32,1024]{2,1,0:T(8,128)(2,1)} %bitcast.34), calls=%async_computation | async-start | bytes 2097152 | tf_op jit(solution)/shard_map/while/body/eval_jaxpr/all_to_all | solution.py:23
Sparse Core Ops, SparseCore 0:
  140.7 12.4 reduce-scatter.4
  268.5 12.4 reduce-scatter.2
where the time goes:
time: 292 us; the launch traced here: 291 us
  blocking collectives  127 us (43%)
  waiting for transfers between devices  102 us (35%)
  matrix products  17.4 us (6%)
  starting transfers between devices  15.7 us (5%)
  between operations  14.1 us (5%)
  local copies, waits for them, and re-layouts  8.85 us (3%)
  other arithmetic  6.44 us (2%)
    all_to_all x4, blocking collectives, accumulate(): lax.all_to_all(col_send, 'tile', split_axis=0, concat_axis=0, tiled=True)  127 us
    all_to_all x4, waiting for transfers between devices, accumulate(): lax.all_to_all(row_send, 'tile', split_axis=0, concat_axis=0, tiled=True)  92.4 us
    dot_general x4, matrix products, accumulate(): lax.dot_general(rows_flat, cols_flat, (((0,), (0,)), ((), ())), preferred...  17.4 us
    all_to_all x4, starting transfers between devices, accumulate(): lax.all_to_all(row_send, 'tile', split_axis=0, concat_axis=0, tiled=True)  15.6 us
    reduce_scatter x2, waiting for transfers between devices, tile_first(): lax.psum_scatter(partial_value, 'grp', scatter_dimension=0, tiled=True)  9.37 us
    mul x2, other arithmetic, hessian_share(): return shares * norm_factor  6.44 us
  transfers between devices with their start and end apart: 6, of which 5 were waited for; matrix products, arithmetic and copies ran while one was open for 5% of the time, Pallas kernels for 0%

commit v1 on v0

--- a/solution.py
+++ b/solution.py
@@ -5,6 +5,22 @@
 
 ROWB = 4
 TOKB = 32
+
+
+def exchange_in_pairs(x, axis, split, join):
+    ways, here = (lax.axis_size(axis), lax.axis_index(axis))
+    width = x.shape[split] // ways
+    shape = list(x.shape)
+    shape[split] = width
+    height = shape[join]
+    shape[join] = height * ways
+    full = jnp.zeros(shape, x.dtype)
+    for mask in range(ways):
+        part = lax.dynamic_slice_in_dim(x, (here ^ mask) * width, width, axis=split)
+        if mask:
+            part = lax.ppermute(part, axis, [(d, d ^ mask) for d in range(ways)])
+        full = lax.dynamic_update_slice_in_dim(full, part, (here ^ mask) * height, axis=join)
+    return full
 
 
 def tile_first(inputs, tile_count):
@@ -21,7 +37,7 @@
         col_send = jnp.tile(col_parts, (ROWB, 1, 1))
         rows_in, cols_in = (
             lax.all_to_all(row_send, "tile", split_axis=0, concat_axis=0, tiled=True),
-            lax.all_to_all(col_send, "tile", split_axis=0, concat_axis=0, tiled=True),
+            exchange_in_pairs(col_send, "tile", 0, 0),
         )
         rows_flat = rows_in.reshape(tile_count * TOKB, row_width)
         cols_flat = cols_in.reshape(tile_count * TOKB, col_width)

time: 292 us -> 266 us (0.911)
  starting transfers between devices: 15.7 us -> 149 us
  blocking collectives: 127 us -> 0 us
  waiting for transfers between devices: 102 us -> 56.4 us
  local copies, waits for them, and re-layouts: 8.85 us -> 20.1 us
    ppermute x0 -> x60, starting transfers between devices: none -> 128 us  [exchange_in_pairs(): part = lax.ppermute(part, axis, [(d, d ^ mask) for d in range(ways)])]
    all_to_all x4 -> x0, blocking collectives: 127 us -> none  [accumulate(): lax.all_to_all(col_send, 'tile', split_axis=0, concat_axis=0, tiled=True)]
    all_to_all x4, waiting for transfers between devices: 92.4 us -> 0.01 us  [accumulate(): lax.all_to_all(row_send, 'tile', split_axis=0, concat_axis=0, tiled=True)]
    ppermute x0 -> x60, waiting for transfers between devices: none -> 48.9 us  [exchange_in_pairs(): part = lax.ppermute(part, axis, [(d, d ^ mask) for d in range(ways)])]
    dynamic_update_slice x0 -> x60, local copies, waits for them, and re-layouts: none -> 8.88 us  [exchange_in_pairs(): lax.dynamic_update_slice_in_dim(full, part, (here ^ mask) * height, axis=...]
    all_to_all x4, starting transfers between devices: 15.6 us -> 20.1 us  [accumulate(): lax.all_to_all(row_send, 'tile', split_axis=0, concat_axis=0, tiled=True)]
  transfers between devices with their start and end apart: 6 -> 66, of which waited for: 5 -> 22; matrix products, arithmetic and copies ran while one was open for 5% -> 10% of each run, Pallas kernels for 0% -> 0%
where the time goes in v1:
time: 266 us; the launch traced here: 264 us
  starting transfers between devices  149 us (56%)
  waiting for transfers between devices  56.4 us (21%)
  local copies, waits for them, and re-layouts  20.1 us (8%)
  matrix products  17.6 us (7%)
  between operations  14.1 us (5%)
  other arithmetic  6.44 us (2%)
    ppermute x60, starting transfers between devices, exchange_in_pairs(): part = lax.ppermute(part, axis, [(d, d ^ mask) for d in range(ways)])  128 us
    ppermute x60, waiting for transfers between devices, exchange_in_pairs(): part = lax.ppermute(part, axis, [(d, d ^ mask) for d in range(ways)])  48.9 us
    all_to_all x4, starting transfers between devices, accumulate(): lax.all_to_all(row_send, 'tile', split_axis=0, concat_axis=0, tiled=True)  20.1 us
    dot_general x4, matrix products, accumulate(): lax.dot_general(rows_flat, cols_flat, (((0,), (0,)), ((), ())), preferred...  17.6 us
    dynamic_update_slice x60, local copies, waits for them, and re-layouts, exchange_in_pairs(): lax.dynamic_update_slice_in_dim(full, part, (here ^ mask) * height, axis=...  8.88 us
    reduce_scatter x2, waiting for transfers between devices, tile_first(): lax.psum_scatter(partial_value, 'grp', scatter_dimension=0, tiled=True)  7.46 us
    mul x2, other arithmetic, hessian_share(): return shares * norm_factor  6.44 us
  transfers between devices with their start and end apart: 66, of which 22 were waited for; matrix products, arithmetic and copies ran while one was open for 10% of the time, Pallas kernels for 0%

profile of v1, /device:TPU:0, one launch (start us, length us, event | category | flops | bytes accessed | tf_op | source)
XLA Modules:
  0.0 264.4 jit_solution(4995387418618076525)
XLA Ops:
  7.2 122.6 %while.29 = (s32[]{:T(128)}, f32[1024,1024]{1,0:T(8,128)}, bf16[64,4096]{1,0:T(8,128)(2,1)}, s32[]{:T(128)}, s32[]{:T(128)}, /*index=5*/s32[]{:T(128)}, s32[]{:T...) while((s32[]{:T(128)}, f32[1024,1024]{1,0:T(8,128)}, ...), condition=%wide.region_4.0_spmd.clone, body=%wide.region_3.0_spmd.clone.sunk | while | flops 1075839104 | bytes 26871544 | solution.py:48
  9.6 8.3 %all-to-all-start.1 = ((bf16[16,32,1024]{2,1,0:T(8,128)(2,1)}), bf16[16,32,1024]{2,1,0:T(8,128)(2,1)S(1)}, u32[]{:S(2)}, u32[]{:S(2)}) async-start(bf16[16,32,1024]{2,1,0:T(8,128)(2,1)} %bitcast.40), calls=%async_computation.1 | async-start | bytes 2097152 | tf_op jit(solution)/shard_map/while/body/eval_jaxpr/all_to_all | solution.py:39
  30.6 4.2 %collective-permute-start.22 = (bf16[1,32,1024]{2,1,0:T(8,128)(2,1)S(1)}, bf16[1,32,1024]{2,1,0:T(8,128)(2,1)S(1)}, u32[]{:S(2)}, u32[]{:S(2)}) collective-permute-start(bf16[1,32,1024]{2,1,0:T(8,128)(2,1)S(1)} %get-tuple-element.294), channel_id=1, source_target_pairs={{0,8},{1,9},{2,10},{3,11},{4,12},{5,13},{6,14},{7,15},{8,0},{9,1},... | collective-permute-start | bytes 196616 | tf_op jit(solution)/shard_map/while/body/eval_jaxpr/ppermute | solution.py:21
  37.5 5.7 %collective-permute-start.23 = (bf16[1,32,1024]{2,1,0:T(8,128)(2,1)S(1)}, bf16[1,32,1024]{2,1,0:T(8,128)(2,1)S(1)}, u32[]{:S(2)}, u32[]{:S(2)}) collective-permute-start(bf16[1,32,1024]{2,1,0:T(8,128)(2,1)S(1)} %get-tuple-element.295), channel_id=1, source_target_pairs={{0,9},{1,8},{2,11},{3,10},{4,13},{5,12},{6,15},{7,14},{8,1},{9,0},... | collective-permute-start | bytes 196616 | tf_op jit(solution)/shard_map/while/body/eval_jaxpr/ppermute | solution.py:21
  48.0 5.9 %collective-permute-done.22 = bf16[1,32,1024]{2,1,0:T(8,128)(2,1)S(1)} collective-permute-done((bf16[1,32,1024]{2,1,0:T(8,128)(2,1)S(1)}, bf16[1,32,1024]{2,1,0:T(8,128)(2,1)S(1)}, u32[]{:S(2)}, u32[]{:S(2)}) %collective-permute-start.22) | collective-permute-done | bytes 65568 | tf_op jit(solution)/shard_map/while/body/eval_jaxpr/ppermute | solution.py:21
  63.5 4.3 %collective-permute-done.29 = bf16[1,32,1024]{2,1,0:T(8,128)(2,1)S(1)} collective-permute-done((bf16[1,32,1024]{2,1,0:T(8,128)(2,1)S(1)}, bf16[1,32,1024]{2,1,0:T(8,128)(2,1)S(1)}, u32[]{:S(2)}, u32[]{:S(2)}) %collective-permute-start.29) | collective-permute-done | bytes 65568 | tf_op jit(solution)/shard_map/while/body/eval_jaxpr/ppermute | solution.py:21
  73.5 3.7 %all-to-all-start.1 = ((bf16[16,32,1024]{2,1,0:T(8,128)(2,1)}), bf16[16,32,1024]{2,1,0:T(8,128)(2,1)S(1)}, u32[]{:S(2)}, u32[]{:S(2)}) async-start(bf16[16,32,1024]{2,1,0:T(8,128)(2,1)} %bitcast.40), calls=%async_computation.1 | async-start | bytes 2097152 | tf_op jit(solution)/shard_map/while/body/eval_jaxpr/all_to_all | solution.py:39
  88.2 3.5 %collective-permute-start.22 = (bf16[1,32,1024]{2,1,0:T(8,128)(2,1)S(1)}, bf16[1,32,1024]{2,1,0:T(8,128)(2,1)S(1)}, u32[]{:S(2)}, u32[]{:S(2)}) collective-permute-start(bf16[1,32,1024]{2,1,0:T(8,128)(2,1)S(1)} %get-tuple-element.294), channel_id=1, source_target_pairs={{0,8},{1,9},{2,10},{3,11},{4,12},{5,13},{6,14},{7,15},{8,0},{9,1},... | collective-permute-start | bytes 196616 | tf_op jit(solution)/shard_map/while/body/eval_jaxpr/ppermute | solution.py:21
  91.7 4.4 %collective-permute-done.18 = bf16[1,32,1024]{2,1,0:T(8,128)(2,1)S(1)} collective-permute-done((bf16[1,32,1024]{2,1,0:T(8,128)(2,1)S(1)}, bf16[1,32,1024]{2,1,0:T(8,128)(2,1)S(1)}, u32[]{:S(2)}, u32[]{:S(2)}) %collective-permute-start.18) | collective-permute-done | bytes 65568 | tf_op jit(solution)/shard_map/while/body/eval_jaxpr/ppermute | solution.py:21
  96.1 6.2 %collective-permute-start.23 = (bf16[1,32,1024]{2,1,0:T(8,128)(2,1)S(1)}, bf16[1,32,1024]{2,1,0:T(8,128)(2,1)S(1)}, u32[]{:S(2)}, u32[]{:S(2)}) collective-permute-start(bf16[1,32,1024]{2,1,0:T(8,128)(2,1)S(1)} %get-tuple-element.295), channel_id=1, source_target_pairs={{0,9},{1,8},{2,11},{3,10},{4,13},{5,12},{6,15},{7,14},{8,1},{9,0},... | collective-permute-start | bytes 196616 | tf_op jit(solution)/shard_map/while/body/eval_jaxpr/ppermute | solution.py:21
  112.8 3.4 %collective-permute-start.28 = (bf16[1,32,1024]{2,1,0:T(8,128)(2,1)S(1)}, bf16[1,32,1024]{2,1,0:T(8,128)(2,1)S(1)}, u32[]{:S(2)}, u32[]{:S(2)}) collective-permute-start(bf16[1,32,1024]{2,1,0:T(8,128)(2,1)S(1)} %get-tuple-element.300), channel_id=1, source_target_pairs={{0,14},{1,15},{2,12},{3,13},{4,10},{5,11},{6,8},{7,9},{8,6},{9,7},... | collective-permute-start | bytes 196616 | tf_op jit(solution)/shard_map/while/body/eval_jaxpr/ppermute | solution.py:21
  120.0 4.3 %collective-permute-done.29 = bf16[1,32,1024]{2,1,0:T(8,128)(2,1)S(1)} collective-permute-done((bf16[1,32,1024]{2,1,0:T(8,128)(2,1)S(1)}, bf16[1,32,1024]{2,1,0:T(8,128)(2,1)S(1)}, u32[]{:S(2)}, u32[]{:S(2)}) %collective-permute-start.29) | collective-permute-done | bytes 65568 | tf_op jit(solution)/shard_map/while/body/eval_jaxpr/ppermute | solution.py:21
  124.3 5.5 %bitcast_add_fusion.5 = f32[1024,1024]{1,0:T(8,128)} fusion(f32[1024,1024]{1,0:T(8,128)} %get-tuple-element.399, bf16[16,32,1024]{2,1,0:T(8,128)(2,1)S(1)} %all-to-all-done.1, bf16[16,32,1024]{2,1,0:T(8,128)(2,1)S(1)} %constant_dynamic-update-slice_fusion.89, pred[]{:T(512)S(6)} %compare.7), kind=kOutput, calls=%fused_computation.33.clone.1 | convolution fusion | flops 1075838976 | bytes 10485761 | tf_op jit(solution)/shard_map/while/body/eval_jaxpr/dot_general | solution.py:44
  130.9 112.8 %while.28 = (s32[]{:T(128)}, f32[1024,1024]{1,0:T(8,128)}, bf16[64,4096]{1,0:T(8,128)(2,1)S(1)}, s32[]{:T(128)}, s32[]{:T(128)}, /*index=5*/s32[]{:T(128)}, s32[...) while((s32[]{:T(128)}, f32[1024,1024]{1,0:T(8,128)}, ...), condition=%wide.region_1.0_spmd.clone, body=%wide.region_0.0_spmd.clone.sunk | while | flops 1075839104 | bytes 26871544 | solution.py:48
  132.3 4.0 %all-to-all-start = ((bf16[16,32,1024]{2,1,0:T(8,128)(2,1)}), bf16[16,32,1024]{2,1,0:T(8,128)(2,1)S(1)}, u32[]{:S(2)}, u32[]{:S(2)}) async-start(bf16[16,32,1024]{2,1,0:T(8,128)(2,1)} %bitcast.34), calls=%async_computation | async-start | bytes 2097152 | tf_op jit(solution)/shard_map/while/body/eval_jaxpr/all_to_all | solution.py:39
  155.5 6.1 %collective-permute-start.8 = (bf16[1,32,1024]{2,1,0:T(8,128)(2,1)S(1)}, bf16[1,32,1024]{2,1,0:T(8,128)(2,1)S(1)}, u32[]{:S(2)}, u32[]{:S(2)}) collective-permute-start(bf16[1,32,1024]{2,1,0:T(8,128)(2,1)S(1)} %get-tuple-element.276), channel_id=1, source_target_pairs={{0,9},{1,8},{2,11},{3,10},{4,13},{5,12},{6,15},{7,14},{8,1},{9,0},... | collective-permute-start | bytes 196616 | tf_op jit(solution)/shard_map/while/body/eval_jaxpr/ppermute | solution.py:21
  167.4 4.8 %collective-permute-start.12 = (bf16[1,32,1024]{2,1,0:T(8,128)(2,1)S(1)}, bf16[1,32,1024]{2,1,0:T(8,128)(2,1)S(1)}, u32[]{:S(2)}, u32[]{:S(2)}) collective-permute-start(bf16[1,32,1024]{2,1,0:T(8,128)(2,1)S(1)} %get-tuple-element.280), channel_id=1, source_target_pairs={{0,13},{1,12},{2,15},{3,14},{4,9},{5,8},{6,11},{7,10},{8,5},{9,4},... | collective-permute-start | bytes 196616 | tf_op jit(solution)/shard_map/while/body/eval_jaxpr/ppermute | solution.py:21
  179.3 3.4 %collective-permute-done.14 = bf16[1,32,1024]{2,1,0:T(8,128)(2,1)S(1)} collective-permute-done((bf16[1,32,1024]{2,1,0:T(8,128)(2,1)S(1)}, bf16[1,32,1024]{2,1,0:T(8,128)(2,1)S(1)}, u32[]{:S(2)}, u32[]{:S(2)}) %collective-permute-start.14) | collective-permute-done | bytes 65568 | tf_op jit(solution)/shard_map/while/body/eval_jaxpr/ppermute | solution.py:21
  187.5 4.1 %all-to-all-start = ((bf16[16,32,1024]{2,1,0:T(8,128)(2,1)}), bf16[16,32,1024]{2,1,0:T(8,128)(2,1)S(1)}, u32[]{:S(2)}, u32[]{:S(2)}) async-start(bf16[16,32,1024]{2,1,0:T(8,128)(2,1)} %bitcast.34), calls=%async_computation | async-start | bytes 2097152 | tf_op jit(solution)/shard_map/while/body/eval_jaxpr/all_to_all | solution.py:39
  210.7 6.2 %collective-permute-start.8 = (bf16[1,32,1024]{2,1,0:T(8,128)(2,1)S(1)}, bf16[1,32,1024]{2,1,0:T(8,128)(2,1)S(1)}, u32[]{:S(2)}, u32[]{:S(2)}) collective-permute-start(bf16[1,32,1024]{2,1,0:T(8,128)(2,1)S(1)} %get-tuple-element.276), channel_id=1, source_target_pairs={{0,9},{1,8},{2,11},{3,10},{4,13},{5,12},{6,15},{7,14},{8,1},{9,0},... | collective-permute-start | bytes 196616 | tf_op jit(solution)/shard_map/while/body/eval_jaxpr/ppermute | solution.py:21
  222.7 4.8 %collective-permute-start.12 = (bf16[1,32,1024]{2,1,0:T(8,128)(2,1)S(1)}, bf16[1,32,1024]{2,1,0:T(8,128)(2,1)S(1)}, u32[]{:S(2)}, u32[]{:S(2)}) collective-permute-start(bf16[1,32,1024]{2,1,0:T(8,128)(2,1)S(1)} %get-tuple-element.280), channel_id=1, source_target_pairs={{0,13},{1,12},{2,15},{3,14},{4,9},{5,8},{6,11},{7,10},{8,5},{9,4},... | collective-permute-start | bytes 196616 | tf_op jit(solution)/shard_map/while/body/eval_jaxpr/ppermute | solution.py:21
  234.6 3.5 %collective-permute-done.14 = bf16[1,32,1024]{2,1,0:T(8,128)(2,1)S(1)} collective-permute-done((bf16[1,32,1024]{2,1,0:T(8,128)(2,1)S(1)}, bf16[1,32,1024]{2,1,0:T(8,128)(2,1)S(1)}, u32[]{:S(2)}, u32[]{:S(2)}) %collective-permute-start.14) | collective-permute-done | bytes 65568 | tf_op jit(solution)/shard_map/while/body/eval_jaxpr/ppermute | solution.py:21
  238.1 5.5 %bitcast_add_fusion.4 = f32[1024,1024]{1,0:T(8,128)} fusion(f32[1024,1024]{1,0:T(8,128)} %get-tuple-element.327, bf16[16,32,1024]{2,1,0:T(8,128)(2,1)S(1)} %all-to-all-done, bf16[16,32,1024]{2,1,0:T(8,128)(2,1)S(1)} %constant_dynamic-update-slice_fusion.74, pred[]{:T(512)S(6)} %compare.6), kind=kOutput, calls=%fused_computation.clone.1 | convolution fusion | flops 1075838976 | bytes 10485761 | tf_op jit(solution)/shard_map/while/body/eval_jaxpr/dot_general | solution.py:44
  246.9 7.4 %reduce-scatter.3.cloned.1.call-done = f32[512,1024]{1,0:T(8,128)} async-done(((f32[1024,1024]{1,0:T(8,128)}), f32[512,1024]{1,0:T(8,128)}) %reduce-scatter.3.cloned.1.call-update) | async-done | bytes 2097168 | tf_op jit(solution)/shard_map/reduce_scatter | solution.py:51
  (210 shorter events, 139.9 us)
Async XLA Ops:
  7.2 236.5 %reduce-scatter.5.cloned.1.call-start = ((), (), s32[]{:S(2)}) async-start(), calls=%async_computation.5 | async-start | bytes 6291456 | tf_op jit(solution)/shard_map/reduce_scatter | solution.py:51
  9.6 58.2 %all-to-all-start.1 = ((bf16[16,32,1024]{2,1,0:T(8,128)(2,1)}), bf16[16,32,1024]{2,1,0:T(8,128)(2,1)S(1)}, u32[]{:S(2)}, u32[]{:S(2)}) async-start(bf16[16,32,1024]{2,1,0:T(8,128)(2,1)} %bitcast.40), calls=%async_computation.1 | async-start | bytes 2097152 | tf_op jit(solution)/shard_map/while/body/eval_jaxpr/all_to_all | solution.py:39
  23.8 19.3 %collective-permute-start.19 = (bf16[1,32,1024]{2,1,0:T(8,128)(2,1)S(1)}, bf16[1,32,1024]{2,1,0:T(8,128)(2,1)S(1)}, u32[]{:S(2)}, u32[]{:S(2)}) collective-permute-start(bf16[1,32,1024]{2,1,0:T(8,128)(2,1)S(1)} %get-tuple-element.291), channel_id=1, source_target_pairs={{0,5},{1,4},{2,7},{3,6},{4,1},{5,0},{6,3},{7,2},{8,13},{9,12},{10,... | collective-permute-start | bytes 196616 | tf_op jit(solution)/shard_map/while/body/eval_jaxpr/ppermute | solution.py:21
  25.3 20.3 %collective-permute-start.20 = (bf16[1,32,1024]{2,1,0:T(8,128)(2,1)S(1)}, bf16[1,32,1024]{2,1,0:T(8,128)(2,1)S(1)}, u32[]{:S(2)}, u32[]{:S(2)}) collective-permute-start(bf16[1,32,1024]{2,1,0:T(8,128)(2,1)S(1)} %get-tuple-element.292), channel_id=1, source_target_pairs={{0,6},{1,7},{2,4},{3,5},{4,2},{5,3},{6,0},{7,1},{8,14},{9,15},{10,... | collective-permute-start | bytes 196616 | tf_op jit(solution)/shard_map/while/body/eval_jaxpr/ppermute | solution.py:21
  29.6 17.6 %collective-permute-start.21 = (bf16[1,32,1024]{2,1,0:T(8,128)(2,1)S(1)}, bf16[1,32,1024]{2,1,0:T(8,128)(2,1)S(1)}, u32[]{:S(2)}, u32[]{:S(2)}) collective-permute-start(bf16[1,32,1024]{2,1,0:T(8,128)(2,1)S(1)} %get-tuple-element.293), channel_id=1, source_target_pairs={{0,7},{1,6},{2,5},{3,4},{4,3},{5,2},{6,1},{7,0},{8,15},{9,14},{10,... | collective-permute-start | bytes 196616 | tf_op jit(solution)/shard_map/while/body/eval_jaxpr/ppermute | solution.py:21
  30.6 23.3 %collective-permute-start.22 = (bf16[1,32,1024]{2,1,0:T(8,128)(2,1)S(1)}, bf16[1,32,1024]{2,1,0:T(8,128)(2,1)S(1)}, u32[]{:S(2)}, u32[]{:S(2)}) collective-permute-start(bf16[1,32,1024]{2,1,0:T(8,128)(2,1)S(1)} %get-tuple-element.294), channel_id=1, source_target_pairs={{0,8},{1,9},{2,10},{3,11},{4,12},{5,13},{6,14},{7,15},{8,0},{9,1},... | collective-permute-start | bytes 196616 | tf_op jit(solution)/shard_map/while/body/eval_jaxpr/ppermute | solution.py:21
  37.5 19.0 %collective-permute-start.23 = (bf16[1,32,1024]{2,1,0:T(8,128)(2,1)S(1)}, bf16[1,32,1024]{2,1,0:T(8,128)(2,1)S(1)}, u32[]{:S(2)}, u32[]{:S(2)}) collective-permute-start(bf16[1,32,1024]{2,1,0:T(8,128)(2,1)S(1)} %get-tuple-element.295), channel_id=1, source_target_pairs={{0,9},{1,8},{2,11},{3,10},{4,13},{5,12},{6,15},{7,14},{8,1},{9,0},... | collective-permute-start | bytes 196616 | tf_op jit(solution)/shard_map/while/body/eval_jaxpr/ppermute | solution.py:21
  73.5 50.8 %all-to-all-start.1 = ((bf16[16,32,1024]{2,1,0:T(8,128)(2,1)}), bf16[16,32,1024]{2,1,0:T(8,128)(2,1)S(1)}, u32[]{:S(2)}, u32[]{:S(2)}) async-start(bf16[16,32,1024]{2,1,0:T(8,128)(2,1)} %bitcast.40), calls=%async_computation.1 | async-start | bytes 2097152 | tf_op jit(solution)/shard_map/while/body/eval_jaxpr/all_to_all | solution.py:39
  83.0 19.4 %collective-permute-start.19 = (bf16[1,32,1024]{2,1,0:T(8,128)(2,1)S(1)}, bf16[1,32,1024]{2,1,0:T(8,128)(2,1)S(1)}, u32[]{:S(2)}, u32[]{:S(2)}) collective-permute-start(bf16[1,32,1024]{2,1,0:T(8,128)(2,1)S(1)} %get-tuple-element.291), channel_id=1, source_target_pairs={{0,5},{1,4},{2,7},{3,6},{4,1},{5,0},{6,3},{7,2},{8,13},{9,12},{10,... | collective-permute-start | bytes 196616 | tf_op jit(solution)/shard_map/while/body/eval_jaxpr/ppermute | solution.py:21
  84.4 20.4 %collective-permute-start.20 = (bf16[1,32,1024]{2,1,0:T(8,128)(2,1)S(1)}, bf16[1,32,1024]{2,1,0:T(8,128)(2,1)S(1)}, u32[]{:S(2)}, u32[]{:S(2)}) collective-permute-start(bf16[1,32,1024]{2,1,0:T(8,128)(2,1)S(1)} %get-tuple-element.292), channel_id=1, source_target_pairs={{0,6},{1,7},{2,4},{3,5},{4,2},{5,3},{6,0},{7,1},{8,14},{9,15},{10,... | collective-permute-start | bytes 196616 | tf_op jit(solution)/shard_map/while/body/eval_jaxpr/ppermute | solution.py:21
  86.9 19.5 %collective-permute-start.21 = (bf16[1,32,1024]{2,1,0:T(8,128)(2,1)S(1)}, bf16[1,32,1024]{2,1,0:T(8,128)(2,1)S(1)}, u32[]{:S(2)}, u32[]{:S(2)}) collective-permute-start(bf16[1,32,1024]{2,1,0:T(8,128)(2,1)S(1)} %get-tuple-element.293), channel_id=1, source_target_pairs={{0,7},{1,6},{2,5},{3,4},{4,3},{5,2},{6,1},{7,0},{8,15},{9,14},{10,... | collective-permute-start | bytes 196616 | tf_op jit(solution)/shard_map/while/body/eval_jaxpr/ppermute | solution.py:21
  88.2 21.5 %collective-permute-start.22 = (bf16[1,32,1024]{2,1,0:T(8,128)(2,1)S(1)}, bf16[1,32,1024]{2,1,0:T(8,128)(2,1)S(1)}, u32[]{:S(2)}, u32[]{:S(2)}) collective-permute-start(bf16[1,32,1024]{2,1,0:T(8,128)(2,1)S(1)} %get-tuple-element.294), channel_id=1, source_target_pairs={{0,8},{1,9},{2,10},{3,11},{4,12},{5,13},{6,14},{7,15},{8,0},{9,1},... | collective-permute-start | bytes 196616 | tf_op jit(solution)/shard_map/while/body/eval_jaxpr/ppermute | solution.py:21
  129.8 124.5 %reduce-scatter.3.cloned.1.call-start = ((), (), s32[]{:S(2)}) async-start(), calls=%async_computation.4 | async-start | bytes 6291456 | tf_op jit(solution)/shard_map/reduce_scatter | solution.py:51
  132.3 50.5 %all-to-all-start = ((bf16[16,32,1024]{2,1,0:T(8,128)(2,1)}), bf16[16,32,1024]{2,1,0:T(8,128)(2,1)S(1)}, u32[]{:S(2)}, u32[]{:S(2)}) async-start(bf16[16,32,1024]{2,1,0:T(8,128)(2,1)} %bitcast.34), calls=%async_computation | async-start | bytes 2097152 | tf_op jit(solution)/shard_map/while/body/eval_jaxpr/all_to_all | solution.py:39
  142.7 19.7 %collective-permute-start.4 = (bf16[1,32,1024]{2,1,0:T(8,128)(2,1)S(1)}, bf16[1,32,1024]{2,1,0:T(8,128)(2,1)}, u32[]{:S(2)}, u32[]{:S(2)}) collective-permute-start(bf16[1,32,1024]{2,1,0:T(8,128)(2,1)S(1)} %get-tuple-element.272), channel_id=1, source_target_pairs={{0,5},{1,4},{2,7},{3,6},{4,1},{5,0},{6,3},{7,2},{8,13},{9,12},{10,... | collective-permute-start | bytes 196616 | tf_op jit(solution)/shard_map/while/body/eval_jaxpr/ppermute | solution.py:21
  144.2 20.7 %collective-permute-start.5 = (bf16[1,32,1024]{2,1,0:T(8,128)(2,1)S(1)}, bf16[1,32,1024]{2,1,0:T(8,128)(2,1)S(1)}, u32[]{:S(2)}, u32[]{:S(2)}) collective-permute-start(bf16[1,32,1024]{2,1,0:T(8,128)(2,1)S(1)} %get-tuple-element.273), channel_id=1, source_target_pairs={{0,6},{1,7},{2,4},{3,5},{4,2},{5,3},{6,0},{7,1},{8,14},{9,15},{10,... | collective-permute-start | bytes 196616 | tf_op jit(solution)/shard_map/while/body/eval_jaxpr/ppermute | solution.py:21
  147.4 19.8 %collective-permute-start.6 = (bf16[1,32,1024]{2,1,0:T(8,128)(2,1)S(1)}, bf16[1,32,1024]{2,1,0:T(8,128)(2,1)S(1)}, u32[]{:S(2)}, u32[]{:S(2)}) collective-permute-start(bf16[1,32,1024]{2,1,0:T(8,128)(2,1)S(1)} %get-tuple-element.274), channel_id=1, source_target_pairs={{0,7},{1,6},{2,5},{3,4},{4,3},{5,2},{6,1},{7,0},{8,15},{9,14},{10,... | collective-permute-start | bytes 196616 | tf_op jit(solution)/shard_map/while/body/eval_jaxpr/ppermute | solution.py:21
  148.5 18.9 %collective-permute-start.7 = (bf16[1,32,1024]{2,1,0:T(8,128)(2,1)S(1)}, bf16[1,32,1024]{2,1,0:T(8,128)(2,1)S(1)}, u32[]{:S(2)}, u32[]{:S(2)}) collective-permute-start(bf16[1,32,1024]{2,1,0:T(8,128)(2,1)S(1)} %get-tuple-element.275), channel_id=1, source_target_pairs={{0,8},{1,9},{2,10},{3,11},{4,12},{5,13},{6,14},{7,15},{8,0},{9,1},... | collective-permute-start | bytes 196616 | tf_op jit(solution)/shard_map/while/body/eval_jaxpr/ppermute | solution.py:21
  187.5 50.7 %all-to-all-start = ((bf16[16,32,1024]{2,1,0:T(8,128)(2,1)}), bf16[16,32,1024]{2,1,0:T(8,128)(2,1)S(1)}, u32[]{:S(2)}, u32[]{:S(2)}) async-start(bf16[16,32,1024]{2,1,0:T(8,128)(2,1)} %bitcast.34), calls=%async_computation | async-start | bytes 2097152 | tf_op jit(solution)/shard_map/while/body/eval_jaxpr/all_to_all | solution.py:39
  198.1 19.7 %collective-permute-start.4 = (bf16[1,32,1024]{2,1,0:T(8,128)(2,1)S(1)}, bf16[1,32,1024]{2,1,0:T(8,128)(2,1)}, u32[]{:S(2)}, u32[]{:S(2)}) collective-permute-start(bf16[1,32,1024]{2,1,0:T(8,128)(2,1)S(1)} %get-tuple-element.272), channel_id=1, source_target_pairs={{0,5},{1,4},{2,7},{3,6},{4,1},{5,0},{6,3},{7,2},{8,13},{9,12},{10,... | collective-permute-start | bytes 196616 | tf_op jit(solution)/shard_map/while/body/eval_jaxpr/ppermute | solution.py:21
  199.9 20.3 %collective-permute-start.5 = (bf16[1,32,1024]{2,1,0:T(8,128)(2,1)S(1)}, bf16[1,32,1024]{2,1,0:T(8,128)(2,1)S(1)}, u32[]{:S(2)}, u32[]{:S(2)}) collective-permute-start(bf16[1,32,1024]{2,1,0:T(8,128)(2,1)S(1)} %get-tuple-element.273), channel_id=1, source_target_pairs={{0,6},{1,7},{2,4},{3,5},{4,2},{5,3},{6,0},{7,1},{8,14},{9,15},{10,... | collective-permute-start | bytes 196616 | tf_op jit(solution)/shard_map/while/body/eval_jaxpr/ppermute | solution.py:21
  202.8 19.8 %collective-permute-start.6 = (bf16[1,32,1024]{2,1,0:T(8,128)(2,1)S(1)}, bf16[1,32,1024]{2,1,0:T(8,128)(2,1)S(1)}, u32[]{:S(2)}, u32[]{:S(2)}) collective-permute-start(bf16[1,32,1024]{2,1,0:T(8,128)(2,1)S(1)} %get-tuple-element.274), channel_id=1, source_target_pairs={{0,7},{1,6},{2,5},{3,4},{4,3},{5,2},{6,1},{7,0},{8,15},{9,14},{10,... | collective-permute-start | bytes 196616 | tf_op jit(solution)/shard_map/while/body/eval_jaxpr/ppermute | solution.py:21
  204.3 18.4 %collective-permute-start.7 = (bf16[1,32,1024]{2,1,0:T(8,128)(2,1)S(1)}, bf16[1,32,1024]{2,1,0:T(8,128)(2,1)S(1)}, u32[]{:S(2)}, u32[]{:S(2)}) collective-permute-start(bf16[1,32,1024]{2,1,0:T(8,128)(2,1)S(1)} %get-tuple-element.275), channel_id=1, source_target_pairs={{0,8},{1,9},{2,10},{3,11},{4,12},{5,13},{6,14},{7,15},{8,0},{9,1},... | collective-permute-start | bytes 196616 | tf_op jit(solution)/shard_map/while/body/eval_jaxpr/ppermute | solution.py:21
  210.7 16.8 %collective-permute-start.8 = (bf16[1,32,1024]{2,1,0:T(8,128)(2,1)S(1)}, bf16[1,32,1024]{2,1,0:T(8,128)(2,1)S(1)}, u32[]{:S(2)}, u32[]{:S(2)}) collective-permute-start(bf16[1,32,1024]{2,1,0:T(8,128)(2,1)S(1)} %get-tuple-element.276), channel_id=1, source_target_pairs={{0,9},{1,8},{2,11},{3,10},{4,13},{5,12},{6,15},{7,14},{8,1},{9,0},... | collective-permute-start | bytes 196616 | tf_op jit(solution)/shard_map/while/body/eval_jaxpr/ppermute | solution.py:21
  (43 other events, 448.5 us)
Sparse Core Ops, SparseCore 0:
  130.0 10.4 reduce-scatter.4
  243.8 10.5 reduce-scatter.2
